TPU v7x, 256 devices: a whole 4x4x8 slice. The times are simulated.
256 devices in a mesh: dp: 8 (over z_lo, core), fsdp: 32 (over y, x, z_hi).
Axes of the slice: x: 4, y: 4, z: 8 (z_hi: 2, z_lo: 4; z = z_hi * 4 + z_lo), core: 2. Of those that a mesh axis runs over, the one named last changes fastest.
Arguments:
- hidden_states: bfloat16 [1024, 4096], P(('dp', 'fsdp')), may hold values from -400 to 400
- token_ids: int32 [1024], P(('dp', 'fsdp')), may hold values from 0 to 4095
- norm_gain: float32 [4096], replicated, may hold values from 0.5 to 1.5
- ref_gate_w: bfloat16 [4096, 14784], P('dp', 'fsdp'), may hold values from -0.1875 to 0.1875
- ref_up_w: bfloat16 [4096, 14784], P('dp', 'fsdp'), may hold values from -0.1875 to 0.1875
- ref_down_w: bfloat16 [14784, 4096], P('fsdp', 'dp'), may hold values from -0.09375 to 0.09375
- pol_gate_w: bfloat16 [4096, 14784], P('dp', 'fsdp'), may hold values from -0.1875 to 0.1875
- pol_up_w: bfloat16 [4096, 14784], P('dp', 'fsdp'), may hold values from -0.1875 to 0.1875
- pol_down_w: bfloat16 [14784, 4096], P('fsdp', 'dp'), may hold values from -0.09375 to 0.09375
- sample_lengths: int32 [8, 32], P('dp'), may hold values from 1 to 24, 128 in all within a row
- prompt_index: int32 [8, 32], P('dp'), may hold values from 0 to 3, as said below
- rewards: float32 [8, 32], P('dp'), may hold values from -6 to 6
Outputs:
- grad_gate: float32 [4096, 14784], P('dp', 'fsdp')
- grad_up: float32 [4096, 14784], P('dp', 'fsdp')
- grad_down: float32 [14784, 4096], P('fsdp', 'dp')
- advantage: float32 [8, 32], P('dp')
Inputs may be any that keep to these rules, and one draw needn't show every extreme that they name: `prompt_index`: in each row, every prompt from 0 to 3 is answered by exactly 8 samples. `sample_lengths`: each row sums to 128.
All inputs are finite; a program needn't handle non-finite values.
Results may differ from a plain program's by a relative error of at most 0.013.
Values may be sent and summed in bfloat16 or wider, within the bound.
A program may use at most 64 MiB of HBM per device.

v0:
```python
import jax
import jax.numpy as jnp
from jax import lax
from jax.sharding import PartitionSpec as P

K = 8
EPSILON = 1e-06
KL_WEIGHT = 0.05


def cut_along(shard, dim, count):
    lengths = shard.shape
    tiles = shard.reshape(*lengths[:dim], count, lengths[dim] // count, *lengths[dim + 1 :])
    return jnp.moveaxis(tiles, dim, 0)


def sent_and_summed(shard, axis, dim):
    tiles = cut_along(shard, dim, lax.axis_size(axis))
    arrived = lax.all_to_all(tiles, axis, split_axis=0, concat_axis=0, tiled=True)
    return arrived.sum(axis=0)


def copy_for_each(shard, axis):
    copies = jnp.broadcast_to(shard, (lax.axis_size(axis), *shard.shape))
    return lax.all_to_all(copies, axis, split_axis=0, concat_axis=0, tiled=True)


def laid_out(tiles, dim):
    lengths = list(tiles.shape[1:])
    lengths[dim] *= tiles.shape[0]
    return jnp.moveaxis(tiles, 0, dim).reshape(lengths)


def gather_directly(shard, axis, dim):
    tiles = copy_for_each(shard, axis)
    return laid_out(tiles, dim)


def all_in_one(shard, axis):
    leaves = jax.tree.leaves(shard)
    sequence = sorted(range(len(leaves)), key=lambda k: -leaves[k].size)
    width = (1, *leaves[sequence[0]].shape)[-1]
    lines = [
        jnp.pad(leaves[k].reshape(-1), (0, -leaves[k].size % width)).reshape(-1, width)
        for k in sequence
    ]
    both, at, found = (copy_for_each(jnp.concatenate(lines), axis), 0, {})
    for k, line in zip(sequence, lines):
        slab = both[:, at : at + len(line)].reshape(len(both), -1)
        found[k] = slab[:, : leaves[k].size].reshape(-1, *leaves[k].shape)
        at += len(line)
    numbers = iter(range(len(leaves)))
    return jax.tree.map(lambda _: found[next(numbers)], shard)


def joined_by_halves(pieces, combine):
    while len(jax.tree.leaves(pieces)[0]) > 1:
        pieces = jax.vmap(combine)(
            *(jax.tree.map(lambda part: part[side::2], pieces) for side in (0, 1))
        )
    return jax.tree.map(lambda part: part[0], pieces)


def joined_all(shard, axis, combine):
    pieces = all_in_one(shard, axis)
    return joined_by_halves(pieces, combine)


def taken_together(shard, axis):
    return copy_for_each(shard, axis).sum(axis=0)


def normalize(states, norm_gain):
    values = states.astype(jnp.float32)
    factor = lax.rsqrt(jnp.mean(values * values, axis=-1, keepdims=True) + EPSILON)
    return (values * factor * norm_gain).astype(jnp.bfloat16)


def combine_totals(first, second):
    row_peak = jnp.maximum(first[0], second[0])
    summed = first[1] * jnp.exp(first[0] - row_peak) + second[1] * jnp.exp(second[0] - row_peak)
    return (row_peak, summed, first[2] + second[2])


def grouped_product(left_rows, right_rows, groups, members):
    group_depth = left_rows.shape[0] // (groups * members)
    left_four = left_rows.reshape(members, groups, group_depth, left_rows.shape[1])
    right_four = right_rows.reshape(members, groups, group_depth, right_rows.shape[1])
    terms = jnp.einsum("jgta,jgtb->gab", left_four, right_four, preferred_element_type=jnp.float32)
    rounded = lax.optimization_barrier(terms.astype(jnp.bfloat16))
    return jnp.sum(rounded.astype(jnp.float32), axis=0)


def column_section(normed_cols, state_cols, ids_all, weight_sets, group_index):
    col_width = state_cols.shape[1]
    unit_count = weight_sets[0][0].shape[1]
    in_weights = jnp.concatenate(
        [matrix for triple in weight_sets for matrix in triple[:2]], axis=1
    )
    pre_sums = sent_and_summed(
        jnp.dot(normed_cols, in_weights, preferred_element_type=jnp.float32), "dp", 0
    )
    activations = []
    for model_index in range(len(weight_sets)):
        gate_pre = pre_sums[:, 2 * model_index * unit_count : (2 * model_index + 1) * unit_count]
        up_pre = pre_sums[
            :, (2 * model_index + 1) * unit_count : (2 * model_index + 2) * unit_count
        ]
        activations.append(jax.nn.silu(gate_pre) * up_pre)
    hidden_local = jnp.concatenate(activations, axis=1).astype(jnp.bfloat16)
    hidden_all = gather_directly(hidden_local, "dp", 0)

    def project_out():
        pieces = [
            jnp.dot(
                hidden_all[:, model_index * unit_count : (model_index + 1) * unit_count],
                weight_sets[model_index][2],
                preferred_element_type=jnp.float32,
            )
            for model_index in range(len(weight_sets))
        ]
        return jnp.concatenate(pieces, axis=1)

    out_cols = sent_and_summed(project_out(), "fsdp", 0)
    states = state_cols.astype(jnp.float32)
    col_ids = jnp.arange(col_width, dtype=jnp.int32) + group_index * col_width
    logits_list = []
    peaks = []
    sums = []
    picks = []
    for model_index in range(len(weight_sets)):
        logits = states + out_cols[:, model_index * col_width : (model_index + 1) * col_width]
        row_peak = jnp.max(logits, axis=1)
        logits_list.append(logits)
        peaks.append(row_peak)
        sums.append(jnp.sum(jnp.exp(logits - row_peak[:, None]), axis=1))
        picks.append(jnp.sum(jnp.where(col_ids[None, :] == ids_all[:, None], logits, 0.0), axis=1))
    row_peak, summed, picked = joined_all(
        (jnp.stack(peaks, axis=1), jnp.stack(sums, axis=1), jnp.stack(picks, axis=1)),
        "dp",
        combine_totals,
    )
    log_total = row_peak + jnp.log(summed)
    return (pre_sums, hidden_all, logits_list, log_total, picked - log_total)


def leave_one_out(log_gap, inside, prompt_index, rewards):
    divergence = taken_together(jnp.sum(log_gap[:, None] * inside, axis=0), "fsdp")
    scores = rewards[0] - KL_WEIGHT * divergence
    same_prompt = (prompt_index[0][:, None] == prompt_index[0][None, :]).astype(jnp.float32)
    others = jnp.sum(same_prompt * scores[None, :], axis=1) - scores
    advantage = scores - others / (K - 1)
    weight = jnp.sum(inside * advantage[None, :], axis=1)
    return (advantage, weight)


def local(
    hidden_states,
    token_ids,
    norm_gain,
    ref_gate_w,
    ref_up_w,
    ref_down_w,
    pol_gate_w,
    pol_up_w,
    pol_down_w,
    sample_lengths,
    prompt_index,
    rewards,
):
    token_count = hidden_states.shape[0]
    groups = lax.axis_size("dp")
    members = lax.axis_size("fsdp")
    group_index = lax.axis_index("dp")
    member_index = lax.axis_index("fsdp")
    unit_count = pol_gate_w.shape[1]
    normed = normalize(hidden_states, norm_gain)
    normed_mixed, state_cols = (
        lax.all_to_all(normed, "dp", split_axis=1, concat_axis=0, tiled=True),
        lax.all_to_all(hidden_states, "dp", split_axis=1, concat_axis=0, tiled=True),
    )
    normed_cols = lax.all_gather(normed_mixed, "fsdp", axis=0, tiled=True)
    ids_all = gather_directly(token_ids, "dp", 0)
    own_start = group_index * token_count
    position = member_index * token_count + jnp.arange(token_count, dtype=jnp.int32)
    sample_ends = jnp.cumsum(sample_lengths[0])
    sample_starts = sample_ends - sample_lengths[0]
    inside = (
        (position[:, None] >= sample_starts[None, :]) & (position[:, None] < sample_ends[None, :])
    ).astype(jnp.float32)
    pre_sums, hidden_all, logits_list, log_total, logprob = column_section(
        normed_cols,
        state_cols,
        ids_all,
        [(ref_gate_w, ref_up_w, ref_down_w), (pol_gate_w, pol_up_w, pol_down_w)],
        group_index,
    )
    ref_own = lax.dynamic_slice_in_dim(logprob[:, 0], own_start, token_count, 0)
    pol_own = lax.dynamic_slice_in_dim(logprob[:, 1], own_start, token_count, 0)
    advantage, weight = leave_one_out(pol_own - ref_own, inside, prompt_index, rewards)
    weight_all = gather_directly(weight, "dp", 0)
    col_width = state_cols.shape[1]
    col_ids = jnp.arange(col_width, dtype=jnp.int32) + group_index * col_width
    onehot_cols = (col_ids[None, :] == ids_all[:, None]).astype(jnp.float32)
    grad_cols = (
        -weight_all[:, None] * (onehot_cols - jnp.exp(logits_list[1] - log_total[:, 1:2]))
    ).astype(jnp.bfloat16)
    grad_cols_all = lax.all_gather(grad_cols, "fsdp", axis=0, tiled=True)
    pol_hidden = hidden_all[:, unit_count : 2 * unit_count]
    grad_down = grouped_product(pol_hidden, grad_cols_all, groups, members)
    grad_hidden = sent_and_summed(
        lax.dot_general(
            grad_cols_all, pol_down_w, (((1,), (1,)), ((), ())), preferred_element_type=jnp.float32
        ),
        "dp",
        0,
    )
    gate_pre = pre_sums[:, 2 * unit_count : 3 * unit_count]
    up_pre = pre_sums[:, 3 * unit_count : 4 * unit_count]
    sigmoid_gate = jax.nn.sigmoid(gate_pre)
    grad_gate_pre = grad_hidden * up_pre * sigmoid_gate * (1.0 + gate_pre * (1.0 - sigmoid_gate))
    grad_up_pre = grad_hidden * gate_pre * sigmoid_gate
    gate_grads = jnp.concatenate(
        [grad_gate_pre.astype(jnp.bfloat16), grad_up_pre.astype(jnp.bfloat16)], axis=1
    )
    gate_grads_all = gather_directly(gate_grads, "dp", 0)
    grad_inner = grouped_product(normed_cols, gate_grads_all, groups, members)
    return (grad_inner[:, :unit_count], grad_inner[:, unit_count:], grad_down, advantage[None, :])


def solution(mesh):
    return jax.shard_map(
        local,
        mesh=mesh,
        in_specs=(
            P(("dp", "fsdp"), None),
            P(("dp", "fsdp")),
            P(),
            P("dp", "fsdp"),
            P("dp", "fsdp"),
            P("fsdp", "dp"),
            P("dp", "fsdp"),
            P("dp", "fsdp"),
            P("fsdp", "dp"),
            P("dp", None),
            P("dp", None),
            P("dp", None),
        ),
        out_specs=(P("dp", "fsdp"), P("dp", "fsdp"), P("fsdp", "dp"), P("dp", None)),
        check_vma=False,
    )
```

profile of v0, /device:TPU:1, one launch (start us, length us, event | category | flops | bytes accessed | tf_op | source)
XLA Modules:
  0.0 705.4 jit_solution(487625159166085097)
XLA Ops:
  7.2 1.0 fusion.7
  8.2 0.9 fusion.9
  9.0 12.2 %all_to_all.80 = bf16[4,8,512]{2,0,1:T(4,128)(2,1)S(1)} all-to-all(bf16[4,8,512]{2,0,1:T(4,128)(2,1)S(1)} %bitcast.86), channel_id=1, replica_groups=mesh['dp'=8,'fsdp'=32] {'dp'}, dimensions={1} | all-to-all | bytes 65536 | tf_op jit(solution)/shard_map/all_to_all | solution.py:179
  21.2 0.6 all_to_all.57
  21.9 8.4 %concatenate.16 = bf16[512,1848]{0,1:T(8,128)(2,1)S(1)} concatenate(bf16[512,462]{0,1:T(8,128)(2,1)} %param.15, bf16[512,462]{0,1:T(8,128)(2,1)} %param.16, bf16[512,462]{0,1:T(8,128)(2,1)} %param.18, bf16[512,462]{0,1:T(8,128)(2,1)} %param.19), dimensions={1} | concatenate | bytes 3784704 | tf_op jit(solution)/shard_map/concatenate | solution.py:97
  30.3 72.1 %all-gather.3.cloned.1.call-done = bf16[1024,512]{1,0:T(8,128)(2,1)} async-done(((bf16[32,512]{1,0:T(8,128)(2,1)}), bf16[1024,512]{1,0:T(8,128)(2,1)}) %all-gather.3.cloned.1.call-update) | async-done | bytes 1048592 | tf_op jit(solution)/shard_map/all_gather | solution.py:182
  102.4 3.4 convolution_bitcast_fusion
  105.8 0.5 copy.105
  106.3 171.0 %all_to_all.81 = f32[8,128,1848]{1,2,0:T(8,128)} all-to-all(f32[8,128,1848]{1,2,0:T(8,128)S(1)} %bitcast.77), channel_id=1, replica_groups=mesh['dp'=8,'fsdp'=32] {'dp'}, dimensions={0} | all-to-all | bytes 15138816 | tf_op jit(solution)/shard_map/all_to_all | solution.py:19
  277.3 3.6 reduce_sum.129
  280.9 0.2 fusion.6
  281.2 0.2 broadcast_in_dim.17
  281.4 47.5 %all_to_all.82 = bf16[8,128,924]{1,2,0:T(8,128)(2,1)S(1)} all-to-all(bf16[8,128,924]{1,2,0:T(8,128)(2,1)S(1)} %broadcast_in_dim.17), channel_id=1, replica_groups=mesh['dp'=8,'fsdp'=32] {'dp'}, dimensions={0} | all-to-all | bytes 3784704 | tf_op jit(solution)/shard_map/all_to_all | solution.py:25
  328.9 0.6 broadcast_in_dim.18
  329.5 4.0 all-to-all-start.5
  333.5 0.7 copy.106
  334.2 0.1 pad.12
  334.3 0.6 copy.93
  334.9 2.1 fusion.27
  337.0 0.8 fusion.4
  337.8 0.5 all-to-all-done.5
  338.3 4.6 all-to-all-start.1
  342.9 4.1 pad_maximum_fusion
  347.0 5.3 copy.74
  352.4 5.0 all-to-all-start.4
  357.7 0.5 broadcast.77
  358.2 0.7 reduce.10
  359.0 102.3 %all-to-all-done.4 = f32[32,32,1024]{2,1,0:T(8,128)} async-done(((f32[32,32,1024]{2,1,0:T(8,128)}), f32[32,32,1024]{2,1,0:T(8,128)}, u32[]{:S(2)}, u32[]{:S(2)}) %all-to-all-start.4) | async-done | bytes 4194336 | tf_op jit(solution)/shard_map/all_to_all | solution.py:19
  461.2 2.4 reduce_sum.130
  463.8 0.2 exponential_reduce_fusion.1
  464.0 0.2 exponential_reduce_fusion
  464.3 0.6 broadcast_in_dim.20
  464.9 4.9 all-to-all-start.6
  469.9 4.9 all-to-all-done.6
  475.1 21.5 %all_to_all.83 = f32[32,1,32]{2,1,0:T(1,128)S(1)} all-to-all(f32[32,1,32]{2,1,0:T(1,128)S(1)} %broadcast_in_dim.21), channel_id=1, replica_groups=mesh['dp'=8,'fsdp'=32] {'fsdp'}, dimensions={0} | all-to-all | bytes 8192 | tf_op jit(solution)/shard_map/all_to_all | solution.py:25
  496.7 0.2 select_reduce_fusion
  496.9 0.1 select_reduce_fusion.1
  497.0 0.6 broadcast_in_dim.22
  497.6 5.3 all-to-all-start.8
  502.9 4.8 all-to-all-done.8
  507.9 0.7 fusion.14
  508.6 74.4 %all-gather.5.cloned.1.call-done = bf16[1024,512]{1,0:T(8,128)(2,1)} async-done(((bf16[32,512]{1,0:T(8,128)(2,1)}), bf16[1024,512]{1,0:T(8,128)(2,1)}) %all-gather.5.cloned.1.call-update) | async-done | bytes 1048592 | tf_op jit(solution)/shard_map/all_gather | solution.py:208
  583.0 1.9 fusion.34
  584.9 0.4 copy.94
  585.4 0.1 slice_bitcast_fusion
  585.5 0.4 copy.76
  585.9 49.0 %all_to_all.84 = f32[8,128,462]{1,2,0:T(8,128)S(1)} all-to-all(f32[8,128,462]{1,2,0:T(8,128)S(1)} %copy.76), channel_id=1, replica_groups=mesh['dp'=8,'fsdp'=32] {'dp'}, dimensions={0} | all-to-all | bytes 3784704 | tf_op jit(solution)/shard_map/all_to_all | solution.py:19
  635.0 0.2 multiply_convert_fusion.1
  635.2 1.5 broadcast_in_dim.44
  636.7 5.2 all-to-all-start.10
  641.9 1.1 reshape.111
  643.0 0.2 slice.150
  643.3 0.5 copy.81
  643.8 1.2 reshape.118
  645.0 1.1 reshape.119
  646.1 0.5 copy-done.6
  646.6 3.6 bitcast_convert_fusion.1
  650.2 1.5 convert_reduce_fusion.1
  651.7 34.2 %all-to-all-done.10 = bf16[8,128,924]{1,2,0:T(8,128)(2,1)} async-done(((bf16[8,128,924]{1,2,0:T(8,128)(2,1)}), bf16[8,128,924]{1,2,0:T(8,128)(2,1)}, u32[]{:S(2)}, u32[]{:S(2)}) %all-to-all-start.10) | async-done | bytes 1892384 | tf_op jit(solution)/shard_map/all_to_all | solution.py:25
  685.9 2.8 copy.78
  688.7 2.2 reshape_reshape.3
  690.9 5.0 bitcast_convert_fusion
  696.0 1.1 convert_reduce_fusion
  697.1 1.5 fusion.31
  (60 shorter events, 1.4 us)
Async XLA Ops:
  7.2 327.7 %copy-start = (bf16[462,512]{1,0:T(8,128)(2,1)S(1)}, bf16[462,512]{1,0:T(8,128)(2,1)}, u32[]{:S(2)}) copy-start(bf16[462,512]{1,0:T(8,128)(2,1)} %param.20) | copy-start | bytes 1419268
  7.2 95.2 %all-gather.3.cloned.1.call-start = ((), (), s32[]{:S(2)}) async-start(), calls=%async_computation.11 | async-start | bytes 1081344 | tf_op jit(solution)/shard_map/all_gather | solution.py:182
  281.4 47.5 %copy-start.9 = (s32[4]{0:T(128)S(1)}, s32[4]{0:T(128)}, u32[]{:S(2)}) copy-start(s32[4]{0:T(128)} %param.13) | copy-start | bytes 52
  329.5 8.8 %all-to-all-start.5 = ((s32[8,1,4]{2,1,0:T(1,128)}), s32[8,1,4]{2,1,0:T(1,128)S(1)}, u32[]{:S(2)}, u32[]{:S(2)}) async-start(s32[8,1,4]{2,1,0:T(1,128)} %broadcast_in_dim.18), calls=%async_computation.5 | async-start | bytes 8192 | tf_op jit(solution)/shard_map/all_to_all | solution.py:25
  334.9 2.1 copy-start.2
  334.9 2.1 copy-start.7
  338.3 14.0 %all-to-all-start.1 = ((bf16[4,8,512]{2,0,1:T(4,128)(2,1)}), bf16[4,8,512]{2,0,1:T(4,128)(2,1)S(1)}, u32[]{:S(2)}, u32[]{:S(2)}) async-start(bf16[4,8,512]{2,0,1:T(4,128)(2,1)} %bitcast.4), calls=%async_computation.1 | async-start | bytes 65536 | tf_op jit(solution)/shard_map/all_to_all | solution.py:180
  352.4 5.0 copy-start.10
  352.4 108.9 %all-to-all-start.4 = ((f32[32,32,1024]{2,1,0:T(8,128)}), f32[32,32,1024]{2,1,0:T(8,128)}, u32[]{:S(2)}, u32[]{:S(2)}) async-start(f32[32,32,1024]{2,1,0:T(8,128)} %bitcast.78), calls=%async_computation.4 | async-start | bytes 8388608 | tf_op jit(solution)/shard_map/all_to_all | solution.py:19
  359.0 137.7 %copy-start.11 = (f32[1,32]{1,0:T(1,128)S(1)}, f32[1,32]{1,0:T(1,128)}, u32[]{:S(2)}) copy-start(f32[1,32]{1,0:T(1,128)} %param.23) | copy-start | bytes 388
  359.0 137.7 %copy-start.8 = (s32[1,32]{1,0:T(1,128)S(1)}, s32[1,32]{1,0:T(1,128)}, u32[]{:S(2)}) copy-start(s32[1,32]{1,0:T(1,128)} %param.22) | copy-start | bytes 388
  464.9 9.8 %all-to-all-start.6 = ((f32[8,96,2]{1,2,0:T(2,128)}), f32[8,96,2]{1,2,0:T(2,128)S(1)}, u32[]{:S(2)}, u32[]{:S(2)}) async-start(f32[8,96,2]{1,2,0:T(2,128)} %broadcast_in_dim.20), calls=%async_computation.6 | async-start | bytes 16384 | tf_op jit(solution)/shard_map/all_to_all | solution.py:25
  496.9 88.5 %copy-start.12 = (f32[1,32]{1,0:T(1,128)}, f32[1,32]{1,0:T(1,128)S(1)}, u32[]{:S(2)}) copy-start(f32[1,32]{1,0:T(1,128)S(1)} %fusion.24) | copy-start | bytes 388
  497.6 10.2 %all-to-all-start.8 = ((f32[8,1,4]{2,1,0:T(1,128)}), f32[8,1,4]{2,1,0:T(1,128)S(1)}, u32[]{:S(2)}, u32[]{:S(2)}) async-start(f32[8,1,4]{2,1,0:T(1,128)} %broadcast_in_dim.22), calls=%async_computation.8 | async-start | bytes 8192 | tf_op jit(solution)/shard_map/all_to_all | solution.py:25
  502.9 80.1 %all-gather.5.cloned.1.call-start = ((), (), s32[]{:S(2)}) async-start(), calls=%async_computation.12 | async-start | bytes 1081344 | tf_op jit(solution)/shard_map/all_gather | solution.py:208
  636.7 5.2 copy-start.5
  636.7 6.3 copy-start.3
  636.7 49.2 %all-to-all-start.10 = ((bf16[8,128,924]{1,2,0:T(8,128)(2,1)}), bf16[8,128,924]{1,2,0:T(8,128)(2,1)}, u32[]{:S(2)}, u32[]{:S(2)}) async-start(bf16[8,128,924]{1,2,0:T(8,128)(2,1)} %broadcast_in_dim.44), calls=%async_computation.10 | async-start | bytes 3801088 | tf_op jit(solution)/shard_map/all_to_all | solution.py:25
  643.2 1.7 copy-start.4
  645.0 1.6 copy-start.6
  696.0 2.6 copy-start.1
Sparse Core Ops, SparseCore 0:
  22.0 80.3 all-gather.2
  508.7 74.2 all-gather.4
where the time goes:
time: 707 us; the launch traced here: 705 us
  blocking collectives  301 us (43%)
  waiting for transfers between devices  293 us (41%)
  local copies, waits for them, and re-layouts  32.9 us (5%)
  starting transfers between devices  29.1 us (4%)
  other arithmetic  17.8 us (3%)
  matrix products  16.8 us (2%)
  between operations  14.4 us (2%)
    all_to_all x2, blocking collectives, sent_and_summed(): lax.all_to_all(tiles, axis, split_axis=0, concat_axis=0, tiled=True)  220 us
    all_to_all x1, waiting for transfers between devices, sent_and_summed(): lax.all_to_all(tiles, axis, split_axis=0, concat_axis=0, tiled=True)  102 us
    all_gather x1, waiting for transfers between devices, local(): grad_cols_all = lax.all_gather(grad_cols, 'fsdp', axis=0, tiled=True)  74.4 us
    all_gather x1, waiting for transfers between devices, local(): normed_cols = lax.all_gather(normed_mixed, 'fsdp', axis=0, tiled=True)  72.1 us
    all_to_all x2, blocking collectives, copy_for_each(): return lax.all_to_all(copies, axis, split_axis=0, concat_axis=0, tiled=True)  69 us
    all_to_all x4, waiting for transfers between devices, copy_for_each(): return lax.all_to_all(copies, axis, split_axis=0, concat_axis=0, tiled=True)  44.5 us
    all_to_all x4, starting transfers between devices, copy_for_each(): return lax.all_to_all(copies, axis, split_axis=0, concat_axis=0, tiled=True)  19.4 us
  transfers between devices with their start and end apart: 8, of which 7 were waited for; matrix products, arithmetic and copies ran while one was open for 5% of the time, Pallas kernels for 0%

commit v1 on v0

--- a/solution.py
+++ b/solution.py
@@ -205,7 +205,10 @@
     grad_cols = (
         -weight_all[:, None] * (onehot_cols - jnp.exp(logits_list[1] - log_total[:, 1:2]))
     ).astype(jnp.bfloat16)
-    grad_cols_all = lax.all_gather(grad_cols, "fsdp", axis=0, tiled=True)
+    size = lax.axis_size("fsdp")
+    tiles_2 = jnp.stack([grad_cols for _ in range(size)])
+    tiles_2 = lax.all_to_all(tiles_2, "fsdp", split_axis=0, concat_axis=0)
+    grad_cols_all = jnp.concatenate(tiles_2, axis=0)
     pol_hidden = hidden_all[:, unit_count : 2 * unit_count]
     grad_down = grouped_product(pol_hidden, grad_cols_all, groups, members)
     grad_hidden = sent_and_summed(

time: 707 us -> 666 us (0.942)
  waiting for transfers between devices: 293 us -> 219 us
  blocking collectives: 301 us -> 335 us
    all_gather x1 -> x0, waiting for transfers between devices: 74.4 us -> none  [local(): grad_cols_all = lax.all_gather(grad_cols, 'fsdp', axis=0, tiled=True)]
    all_to_all x0 -> x1, blocking collectives: none -> 30.2 us  [local(): tiles_2 = lax.all_to_all(tiles_2, 'fsdp', split_axis=0, concat_axis=0)]
  transfers between devices with their start and end apart: 8 -> 7, of which waited for: 7 -> 6; matrix products, arithmetic and copies ran while one was open for 5% -> 5% of each run, Pallas kernels for 0% -> 0%
where the time goes in v1:
time: 666 us; the launch traced here: 664 us
  blocking collectives  335 us (50%)
  waiting for transfers between devices  219 us (33%)
  local copies, waits for them, and re-layouts  35.3 us (5%)
  starting transfers between devices  29 us (4%)
  other arithmetic  19 us (3%)
  between operations  14.4 us (2%)
  matrix products  13.2 us (2%)
    all_to_all x2, blocking collectives, sent_and_summed(): lax.all_to_all(tiles, axis, split_axis=0, concat_axis=0, tiled=True)  224 us
    all_to_all x1, waiting for transfers between devices, sent_and_summed(): lax.all_to_all(tiles, axis, split_axis=0, concat_axis=0, tiled=True)  102 us
    all_gather x1, waiting for transfers between devices, local(): normed_cols = lax.all_gather(normed_mixed, 'fsdp', axis=0, tiled=True)  72.1 us
    all_to_all x2, blocking collectives, copy_for_each(): return lax.all_to_all(copies, axis, split_axis=0, concat_axis=0, tiled=True)  69 us
    all_to_all x4, waiting for transfers between devices, copy_for_each(): return lax.all_to_all(copies, axis, split_axis=0, concat_axis=0, tiled=True)  44.3 us
    all_to_all x1, blocking collectives, local(): tiles_2 = lax.all_to_all(tiles_2, 'fsdp', split_axis=0, concat_axis=0)  30.2 us
    all_to_all x4, starting transfers between devices, copy_for_each(): return lax.all_to_all(copies, axis, split_axis=0, concat_axis=0, tiled=True)  19.3 us
  transfers between devices with their start and end apart: 7, of which 6 were waited for; matrix products, arithmetic and copies ran while one was open for 5% of the time, Pallas kernels for 0%

profile of v1, /device:TPU:1, one launch (start us, length us, event | category | flops | bytes accessed | tf_op | source)
XLA Modules:
  0.0 664.5 jit_solution(15630877110212280386)
XLA Ops:
  7.2 1.0 fusion.8
  8.2 0.9 fusion.10
  9.0 12.2 %all_to_all.85 = bf16[4,8,512]{2,0,1:T(4,128)(2,1)S(1)} all-to-all(bf16[4,8,512]{2,0,1:T(4,128)(2,1)S(1)} %bitcast.85), channel_id=1, replica_groups=mesh['dp'=8,'fsdp'=32] {'dp'}, dimensions={1} | all-to-all | bytes 65536 | tf_op jit(solution)/shard_map/all_to_all | solution.py:179
  21.2 0.6 all_to_all.60
  21.8 8.4 %concatenate.16 = bf16[512,1848]{0,1:T(8,128)(2,1)S(1)} concatenate(bf16[512,462]{0,1:T(8,128)(2,1)} %param.15, bf16[512,462]{0,1:T(8,128)(2,1)} %param.16, bf16[512,462]{0,1:T(8,128)(2,1)} %param.18, bf16[512,462]{0,1:T(8,128)(2,1)} %param.19), dimensions={1} | concatenate | bytes 3784704 | tf_op jit(solution)/shard_map/concatenate | solution.py:97
  30.3 72.1 %all-gather.2.cloned.1.call-done = bf16[1024,512]{1,0:T(8,128)(2,1)} async-done(((bf16[32,512]{1,0:T(8,128)(2,1)}), bf16[1024,512]{1,0:T(8,128)(2,1)}) %all-gather.2.cloned.1.call-update) | async-done | bytes 1048592 | tf_op jit(solution)/shard_map/all_gather | solution.py:182
  102.4 3.4 convolution_bitcast_fusion
  105.8 0.5 copy.94
  106.3 171.0 %all_to_all.86 = f32[8,128,1848]{1,2,0:T(8,128)} all-to-all(f32[8,128,1848]{1,2,0:T(8,128)S(1)} %bitcast.76), channel_id=1, replica_groups=mesh['dp'=8,'fsdp'=32] {'dp'}, dimensions={0} | all-to-all | bytes 15138816 | tf_op jit(solution)/shard_map/all_to_all | solution.py:19
  277.3 3.6 reduce_sum.129
  280.9 0.2 fusion.7
  281.2 0.7 copy-done.3
  281.9 0.2 broadcast_in_dim.17
  282.1 47.5 %all_to_all.87 = bf16[8,128,924]{1,2,0:T(8,128)(2,1)S(1)} all-to-all(bf16[8,128,924]{1,2,0:T(8,128)(2,1)S(1)} %broadcast_in_dim.17), channel_id=1, replica_groups=mesh['dp'=8,'fsdp'=32] {'dp'}, dimensions={0} | all-to-all | bytes 3784704 | tf_op jit(solution)/shard_map/all_to_all | solution.py:25
  329.6 0.6 broadcast_in_dim.18
  330.2 4.0 all-to-all-start.5
  334.2 0.7 copy.95
  334.9 0.1 pad.12
  335.0 0.6 copy.85
  335.6 2.1 fusion.28
  337.7 0.8 fusion.3
  338.5 0.5 all-to-all-done.5
  339.0 4.6 all-to-all-start.1
  343.6 4.1 pad_maximum_fusion
  347.7 5.3 copy.69
  353.1 5.0 all-to-all-start.4
  358.2 0.1 reduce.1
  358.4 0.5 broadcast.79
  358.9 0.7 reduce.10
  359.7 102.3 %all-to-all-done.4 = f32[32,32,1024]{2,1,0:T(8,128)} async-done(((f32[32,32,1024]{2,1,0:T(8,128)}), f32[32,32,1024]{2,1,0:T(8,128)}, u32[]{:S(2)}, u32[]{:S(2)}) %all-to-all-start.4) | async-done | bytes 4194336 | tf_op jit(solution)/shard_map/all_to_all | solution.py:19
  462.0 2.4 reduce_sum.130
  464.4 0.1 fusion.27
  464.5 0.2 exponential_reduce_fusion.1
  464.7 0.2 exponential_reduce_fusion
  465.0 0.6 broadcast_in_dim.20
  465.6 4.9 all-to-all-start.6
  470.6 4.9 all-to-all-done.6
  475.8 21.5 %all_to_all.88 = f32[32,1,32]{2,1,0:T(1,128)S(1)} all-to-all(f32[32,1,32]{2,1,0:T(1,128)S(1)} %broadcast_in_dim.21), channel_id=1, replica_groups=mesh['dp'=8,'fsdp'=32] {'fsdp'}, dimensions={0} | all-to-all | bytes 8192 | tf_op jit(solution)/shard_map/all_to_all | solution.py:25
  497.4 0.2 select_reduce_fusion
  497.6 0.1 select_reduce_fusion.1
  497.7 0.6 broadcast_in_dim.22
  498.3 5.3 all-to-all-start.8
  503.7 4.8 all-to-all-done.8
  508.8 30.2 %all_to_all.89 = bf16[32,32,512]{2,1,0:T(8,128)(2,1)S(1)} all-to-all(bf16[32,32,512]{2,1,0:T(8,128)(2,1)S(1)} %stack.29), channel_id=1, replica_groups=mesh['dp'=8,'fsdp'=32] {'fsdp'}, dimensions={0} | all-to-all | bytes 2097152 | tf_op jit(solution)/shard_map/all_to_all | solution.py:210
  539.0 0.7 fusion.5
  539.7 52.6 %all_to_all.90 = f32[8,128,462]{1,2,0:T(8,128)S(1)} all-to-all(f32[8,128,462]{1,2,0:T(8,128)S(1)} %fusion.5), channel_id=1, replica_groups=mesh['dp'=8,'fsdp'=32] {'dp'}, dimensions={0} | all-to-all | bytes 3784704 | tf_op jit(solution)/shard_map/all_to_all | solution.py:19
  592.3 0.8 reduce_sum.140
  593.1 1.3 multiply_convert_fusion.1
  594.4 1.5 broadcast_in_dim.44
  595.9 5.1 all-to-all-start.11
  601.0 2.2 reshape.111
  603.2 1.2 slice.150
  604.3 1.5 copy.74
  605.8 1.2 reshape.117
  607.0 0.6 copy.75
  607.6 0.6 copy-done.4
  608.2 1.2 bitcast_convert_fusion.1
  609.4 1.5 convert_reduce_fusion.1
  610.9 34.1 %all-to-all-done.11 = bf16[8,128,924]{1,2,0:T(8,128)(2,1)} async-done(((bf16[8,128,924]{1,2,0:T(8,128)(2,1)}), bf16[8,128,924]{1,2,0:T(8,128)(2,1)}, u32[]{:S(2)}, u32[]{:S(2)}) %all-to-all-start.11) | async-done | bytes 1892384 | tf_op jit(solution)/shard_map/all_to_all | solution.py:25
  645.0 2.8 copy.71
  647.8 2.2 reshape_reshape.6
  650.0 5.0 bitcast_convert_fusion
  655.1 1.1 convert_reduce_fusion
  656.2 1.5 fusion.32
  (52 shorter events, 1.2 us)
Async XLA Ops:
  7.2 328.4 %copy-start = (bf16[462,512]{1,0:T(8,128)(2,1)S(1)}, bf16[462,512]{1,0:T(8,128)(2,1)}, u32[]{:S(2)}) copy-start(bf16[462,512]{1,0:T(8,128)(2,1)} %param.20) | copy-start | bytes 1419268
  7.2 95.2 %all-gather.2.cloned.1.call-start = ((), (), s32[]{:S(2)}) async-start(), calls=%async_computation.12 | async-start | bytes 1081344 | tf_op jit(solution)/shard_map/all_gather | solution.py:182
  280.9 0.9 copy-start.3
  282.1 47.5 %copy-start.7 = (s32[4]{0:T(128)S(1)}, s32[4]{0:T(128)}, u32[]{:S(2)}) copy-start(s32[4]{0:T(128)} %param.13) | copy-start | bytes 52
  330.2 8.8 %all-to-all-start.5 = ((s32[8,1,4]{2,1,0:T(1,128)}), s32[8,1,4]{2,1,0:T(1,128)S(1)}, u32[]{:S(2)}, u32[]{:S(2)}) async-start(s32[8,1,4]{2,1,0:T(1,128)} %broadcast_in_dim.18), calls=%async_computation.5 | async-start | bytes 8192 | tf_op jit(solution)/shard_map/all_to_all | solution.py:25
  335.6 2.1 copy-start.1
  335.6 2.1 copy-start.5
  339.0 14.1 %all-to-all-start.1 = ((bf16[4,8,512]{2,0,1:T(4,128)(2,1)}), bf16[4,8,512]{2,0,1:T(4,128)(2,1)S(1)}, u32[]{:S(2)}, u32[]{:S(2)}) async-start(bf16[4,8,512]{2,0,1:T(4,128)(2,1)} %bitcast.4), calls=%async_computation.1 | async-start | bytes 65536 | tf_op jit(solution)/shard_map/all_to_all | solution.py:180
  353.1 5.0 copy-start.8
  353.1 108.9 %all-to-all-start.4 = ((f32[32,32,1024]{2,1,0:T(8,128)}), f32[32,32,1024]{2,1,0:T(8,128)}, u32[]{:S(2)}, u32[]{:S(2)}) async-start(f32[32,32,1024]{2,1,0:T(8,128)} %bitcast.77), calls=%async_computation.4 | async-start | bytes 8388608 | tf_op jit(solution)/shard_map/all_to_all | solution.py:19
  359.7 137.7 %copy-start.9 = (f32[1,32]{1,0:T(1,128)S(1)}, f32[1,32]{1,0:T(1,128)}, u32[]{:S(2)}) copy-start(f32[1,32]{1,0:T(1,128)} %param.23) | copy-start | bytes 388
  359.7 137.7 %copy-start.6 = (s32[1,32]{1,0:T(1,128)S(1)}, s32[1,32]{1,0:T(1,128)}, u32[]{:S(2)}) copy-start(s32[1,32]{1,0:T(1,128)} %param.22) | copy-start | bytes 388
  465.6 9.8 %all-to-all-start.6 = ((f32[8,96,2]{1,2,0:T(2,128)}), f32[8,96,2]{1,2,0:T(2,128)S(1)}, u32[]{:S(2)}, u32[]{:S(2)}) async-start(f32[8,96,2]{1,2,0:T(2,128)} %broadcast_in_dim.20), calls=%async_computation.6 | async-start | bytes 16384 | tf_op jit(solution)/shard_map/all_to_all | solution.py:25
  497.6 42.1 %copy-start.10 = (f32[1,32]{1,0:T(1,128)}, f32[1,32]{1,0:T(1,128)S(1)}, u32[]{:S(2)}) copy-start(f32[1,32]{1,0:T(1,128)S(1)} %fusion.25) | copy-start | bytes 388
  498.3 10.2 %all-to-all-start.8 = ((f32[8,1,4]{2,1,0:T(1,128)}), f32[8,1,4]{2,1,0:T(1,128)S(1)}, u32[]{:S(2)}, u32[]{:S(2)}) async-start(f32[8,1,4]{2,1,0:T(1,128)} %broadcast_in_dim.22), calls=%async_computation.8 | async-start | bytes 8192 | tf_op jit(solution)/shard_map/all_to_all | solution.py:25
  595.9 7.2 %copy-start.2 = (bf16[116,8,8,128]{3,1,2,0:T(8,128)(2,1)S(1)}, bf16[116,8,8,128]{3,1,2,0:T(8,128)(2,1)}, u32[]{:S(2)}) copy-start(bf16[116,8,8,128]{3,1,2,0:T(8,128)(2,1)} %copy-done.1) | copy-start | bytes 5701636
  595.9 49.1 %all-to-all-start.11 = ((bf16[8,128,924]{1,2,0:T(8,128)(2,1)}), bf16[8,128,924]{1,2,0:T(8,128)(2,1)}, u32[]{:S(2)}, u32[]{:S(2)}) async-start(bf16[8,128,924]{1,2,0:T(8,128)(2,1)} %broadcast_in_dim.44), calls=%async_computation.11 | async-start | bytes 3801088 | tf_op jit(solution)/shard_map/all_to_all | solution.py:25
  607.0 1.2 copy-start.4
Sparse Core Ops, SparseCore 0:
  22.0 80.3 all-gather.1
